TPU v7x, 256 devices: a whole 4x4x8 slice. The times are simulated.
256 devices in a mesh: expert: 32 (over y, x, core), dp: 8 (over z).
Axes of the slice: x: 4, y: 4, z: 8, core: 2. Of those that a mesh axis runs over, the one named last changes fastest.
Arguments:
- tokens: bfloat16 [49152, 1024], P(('expert', 'dp')), may hold values from -6 to 6
- grad_out: bfloat16 [49152, 1024], P(('expert', 'dp')), may hold values from -6 to 6
- routes: int32 [49152, 2], P(('expert', 'dp')), may hold values from 0 to 31, all different within a row
- keep_second: int32 [49152], P(('expert', 'dp')), may hold values 0 or 1
- combine: bfloat16 [49152, 2], P(('expert', 'dp')), may hold values from 0.099609375 to 0.8984375
- w_in: bfloat16 [32, 2048, 1024], P('expert'), may hold values from -0.1875 to 0.1875
- w_out: bfloat16 [32, 2048, 1024], P('expert'), may hold values from -0.125 to 0.125
Outputs:
- grad_tokens: bfloat16 [49152, 1024], P(('expert', 'dp'))
- grad_combine: bfloat16 [49152, 2], P(('expert', 'dp'))
- grad_w_in: float32 [32, 2048, 1024], P('expert', 'dp')
- grad_w_out: float32 [32, 2048, 1024], P('expert', 'dp')
Inputs may be any that keep to these rules, and one draw needn't show every extreme that they name: `routes`: each token names two different experts.
All inputs are finite; a program needn't handle non-finite values. No bound on the sum of `keep_second` on one device may be relied on, other than what follows from the above.
Results may differ from a plain program's by a relative error of at most 0.011.
Values may be sent and summed in bfloat16 or wider, within the bound.
A program may use at most 128 MiB of HBM per device.

v0:
```python
import math

import jax
import jax.numpy as jnp
from jax import lax
from jax.sharding import PartitionSpec as P

root_coef = 0.7978845608
cube_coef = 0.044715


def side_by_side(arrays, axis, split_dim, concat_dim, along):
    widths = [math.prod(a.shape[along:]) for a in arrays]
    both = jnp.concatenate(
        [a.reshape(*a.shape[:along], w) for a, w in zip(arrays, widths)], axis=along
    )
    result = lax.all_to_all(both, axis, split_axis=split_dim, concat_axis=concat_dim, tiled=True)
    pieces = jnp.split(result, [sum(widths[:k]) for k in range(1, len(widths))], axis=along)
    return tuple(
        (b.reshape(*result.shape[:along], *a.shape[along:]) for a, b in zip(arrays, pieces))
    )


def gelu_slope(hidden):
    inner_arg = root_coef * (hidden + cube_coef * hidden * hidden * hidden)
    tanh_val = jnp.tanh(inner_arg)
    active = 0.5 * hidden * (1.0 + tanh_val)
    derivative = 0.5 * (1.0 + tanh_val) + 0.5 * hidden * (1.0 - tanh_val * tanh_val) * root_coef * (
        1.0 + 3.0 * cube_coef * hidden * hidden
    )
    return (active, derivative)


def slot_index(routes, keep_second, expert_count, capacity):
    expert_ids = jnp.arange(expert_count, dtype=jnp.int32)
    first_hot = (routes[:, 0:1] == expert_ids[None, :]).astype(jnp.int32)
    second_hot = (routes[:, 1:2] == expert_ids[None, :]).astype(jnp.int32) * keep_second[:, None]
    first_pos = jnp.cumsum(first_hot, axis=0) - first_hot
    second_pos = jnp.cumsum(second_hot, axis=0) - second_hot + jnp.sum(first_hot, axis=0)[None, :]
    first_slot = jnp.sum(first_pos * first_hot, axis=1)
    second_slot = jnp.sum(second_pos * second_hot, axis=1)
    first_flat = jnp.where(first_slot < capacity, routes[:, 0] * capacity + first_slot, -1)
    second_live = (keep_second > 0) & (second_slot < capacity)
    second_flat = jnp.where(second_live, routes[:, 1] * capacity + second_slot, -1)
    slot_ids = jnp.arange(expert_count * capacity, dtype=jnp.int32)
    first_pick = slot_ids[:, None] == first_flat[None, :]
    second_pick = slot_ids[:, None] == second_flat[None, :]
    return (first_pick, second_pick)


def dispatch(tokens, grad_out, combine, first_pick, second_pick):
    chosen = (first_pick | second_pick).astype(jnp.bfloat16)
    sent_x = jnp.dot(chosen, tokens, preferred_element_type=jnp.float32).astype(jnp.bfloat16)
    sent_dy = jnp.dot(chosen, grad_out, preferred_element_type=jnp.float32).astype(jnp.bfloat16)
    weights = combine.astype(jnp.float32)
    sent_c = jnp.sum(
        jnp.where(first_pick, weights[None, :, 0], 0.0)
        + jnp.where(second_pick, weights[None, :, 1], 0.0),
        axis=1,
    ).astype(jnp.bfloat16)
    return (sent_x, sent_dy, sent_c)


def expert_rows(rows_x, rows_dy, rows_c, weight_in, weight_out):
    hidden = lax.dot_general(
        rows_x, weight_in, (((1,), (1,)), ((), ())), preferred_element_type=jnp.float32
    )
    active, derivative = gelu_slope(hidden)
    active_b = active.astype(jnp.bfloat16)
    output = jnp.dot(active_b, weight_out, preferred_element_type=jnp.float32)
    gate_grad = jnp.sum(output * rows_dy.astype(jnp.float32), axis=1).astype(jnp.bfloat16)
    scaled = (rows_c.astype(jnp.float32)[:, None] * rows_dy.astype(jnp.float32)).astype(
        jnp.bfloat16
    )
    active_grad = lax.dot_general(
        scaled, weight_out, (((1,), (1,)), ((), ())), preferred_element_type=jnp.float32
    )
    hidden_grad = (active_grad * derivative).astype(jnp.bfloat16)
    token_grad = jnp.dot(hidden_grad, weight_in, preferred_element_type=jnp.float32).astype(
        jnp.bfloat16
    )
    return (token_grad, gate_grad, hidden_grad, active_b, scaled)


def collect(token_back, gate_back, first_pick, second_pick):
    chosen = (first_pick | second_pick).astype(jnp.bfloat16)
    grad_tokens = lax.dot_general(
        chosen, token_back, (((0,), (0,)), ((), ())), preferred_element_type=jnp.float32
    ).astype(jnp.bfloat16)
    gate_float = gate_back.astype(jnp.float32)[:, None]
    first_grad = jnp.sum(jnp.where(first_pick, gate_float, 0.0), axis=0)
    second_grad = jnp.sum(jnp.where(second_pick, gate_float, 0.0), axis=0)
    grad_combine = jnp.stack([first_grad, second_grad], axis=1).astype(jnp.bfloat16)
    return (grad_tokens, grad_combine)


def per_device(tokens, grad_out, routes, keep_second, combine, w_in, w_out):
    expert_count = lax.axis_size("expert")
    tok_rows = tokens.shape[0]
    model_width = tokens.shape[1]
    capacity = 5 * tok_rows // (2 * expert_count)
    first_pick, second_pick = slot_index(routes, keep_second, expert_count, capacity)
    sent_x, sent_dy, sent_c = dispatch(tokens, grad_out, combine, first_pick, second_pick)
    sent_x = sent_x.reshape(expert_count, capacity, model_width)
    sent_dy = sent_dy.reshape(expert_count, capacity, model_width)
    sent_c = sent_c.reshape(expert_count, capacity)
    weight_in = w_in[0]
    weight_out = w_out[0]
    got_x, got_dy, got_c = side_by_side((sent_x, sent_dy, sent_c), "expert", 0, 0, 2)
    sources = got_c.shape[0]
    rows_x = got_x.reshape(sources * capacity, model_width)
    token_grad, gate_grad, hidden_grad, active_b, scaled = expert_rows(
        rows_x,
        got_dy.reshape(sources * capacity, model_width),
        got_c.reshape(sources * capacity),
        weight_in,
        weight_out,
    )
    token_back, gate_back = side_by_side(
        (token_grad.reshape(sources, capacity, model_width), gate_grad.reshape(sources, capacity)),
        "expert",
        0,
        0,
        2,
    )
    token_back = token_back.reshape(expert_count * capacity, model_width)
    gate_back = gate_back.reshape(expert_count * capacity)
    term_in = lax.dot_general(
        hidden_grad, rows_x, (((0,), (0,)), ((), ())), preferred_element_type=jnp.float32
    )
    term_out = lax.dot_general(
        active_b, scaled, (((0,), (0,)), ((), ())), preferred_element_type=jnp.float32
    )
    summed = lax.psum_scatter(
        jnp.concatenate([term_in, term_out], axis=1).astype(jnp.bfloat16),
        "dp",
        scatter_dimension=0,
        tiled=True,
    ).astype(jnp.float32)
    grad_in = summed[:, :model_width]
    grad_outw = summed[:, model_width:]
    grad_tokens, grad_combine = collect(token_back, gate_back, first_pick, second_pick)
    return (grad_tokens, grad_combine, grad_in[None], grad_outw[None])


def solution(mesh):
    return jax.shard_map(
        per_device,
        mesh=mesh,
        in_specs=(
            P(("expert", "dp"), None),
            P(("expert", "dp"), None),
            P(("expert", "dp"), None),
            P(("expert", "dp")),
            P(("expert", "dp"), None),
            P("expert", None, None),
            P("expert", None, None),
        ),
        out_specs=(
            P(("expert", "dp"), None),
            P(("expert", "dp"), None),
            P("expert", "dp", None),
            P("expert", "dp", None),
        ),
        check_vma=False,
    )
```

profile of v0, /device:TPU:2, one launch (start us, length us, event | category | flops | bytes accessed | tf_op | source)
XLA Modules:
  0.0 195.9 jit_solution(16687348809667211594)
XLA Ops:
  7.2 0.8 fusion.40
  8.0 0.8 fusion.41
  8.8 0.6 reduce-window.14
  9.4 0.2 slice_reduce_fusion.1
  9.7 0.1 fusion.35
  9.8 0.7 fusion.38
  10.5 0.6 reduce-window.16
  11.1 0.2 slice_reduce_fusion
  11.4 0.8 fusion.37
  12.2 0.7 and_select_fusion
  12.9 0.2 add_reduce_fusion
  13.1 0.9 convert_element_type.132
  14.0 0.6 convolution_convert_fusion.2
  14.5 0.3 reshape.112
  14.8 1.6 convolution_convert_fusion.3
  16.4 0.3 reshape.111
  16.7 1.1 pad_maximum_fusion.1
  17.9 36.5 %all_to_all.10 = bf16[32,15,2049]{2,1,0:T(8,128)(2,1)S(1)} all-to-all(bf16[32,15,2049]{2,1,0:T(8,128)(2,1)S(1)} %pad_maximum_fusion.1), channel_id=1, replica_groups=mesh['expert'=32,'dp'=8] {'expert'}, dimensions={0} | all-to-all | bytes 3934080 | tf_op jit(solution)/shard_map/all_to_all | solution.py:17
  54.4 0.1 fusion.33
  54.5 0.1 reshape.120
  54.7 0.3 copy.33
  54.9 1.2 multiply_convert_fusion.1
  56.2 2.3 %convert_element_type.113 = bf16[480,1024]{1,0:T(8,128)(2,1)} reshape(bf16[32,15,1024]{2,1,0:T(8,128)(2,1)} %multiply_convert_fusion.1) | data formatting | bytes 1966080 | tf_op jit(solution)/shard_map/convert_element_type | solution.py:72
  58.5 2.0 %fusion.39 = (bf16[32,15,1024]{2,1,0:T(8,128)(2,1)}, f32[32,15,1024]{2,1,0:T(8,128)}) fusion(bf16[32,15,2049]{2,1,0:T(8,128)(2,1)S(1)} %all_to_all.10), kind=kLoop, calls=%fused_computation.75 | loop fusion | flops 491520 | bytes 4915200 | tf_op jit(solution)/shard_map/split | solution.py:18
  60.5 1.5 reshape.113
  62.0 1.7 reshape.118
  63.7 4.6 %fusion.2 = f32[480,2048]{1,0:T(8,128)S(1)} fusion(bf16[480,1024]{1,0:T(8,128)(2,1)S(1)} %reshape.113, bf16[1,2048,1024]{2,1,0:T(8,128)(2,1)} %param.12), kind=kOutput, calls=%fused_computation.5 | convolution fusion | flops 2013265920 | bytes 9109504 | tf_op jit(solution)/shard_map/dot_general | solution.py:65
  68.4 4.2 %fusion.14 = bf16[480,2048]{1,0:T(8,128)(2,1)S(1)} fusion(f32[480,2048]{1,0:T(8,128)S(1)} %fusion.2, bf16[480,1024]{1,0:T(8,128)(2,1)S(1)} %copy-done.1, bf16[1,2048,1024]{2,1,0:T(8,128)(2,1)S(1)} %copy-done.2), kind=kOutput, calls=%fused_computation.17 | convolution fusion | flops 2031943680 | bytes 11075584 | tf_op jit(solution)/shard_map/dot_general | solution.py:75
  72.6 4.4 %convolution_convert_fusion.1 = bf16[2048,1024]{0,1:T(8,128)(2,1)} fusion(bf16[480,2048]{1,0:T(8,128)(2,1)S(1)} %fusion.14, bf16[480,1024]{1,0:T(8,128)(2,1)S(1)} %reshape.113), kind=kOutput, calls=%fused_computation.20 | convolution fusion | flops 2015363072 | bytes 7143424 | tf_op jit(solution)/shard_map/dot_general | solution.py:128
  77.0 4.3 %convolution_convert_fusion = bf16[2048,1024]{0,1:T(8,128)(2,1)} fusion(f32[480,1024]{1,0:T(8,128)S(1)} %reshape.118, f32[480]{0:T(512)S(1)} %reshape.120, f32[480,2048]{1,0:T(8,128)S(1)} %fusion.2), kind=kOutput, calls=%fused_computation.19 | convolution fusion | flops 2025193472 | bytes 10094464 | tf_op jit(solution)/shard_map/dot_general | solution.py:131
  81.3 8.4 %pad_maximum_fusion = bf16[2048,2048]{0,1:T(8,128)(2,1)} fusion(bf16[2048,1024]{0,1:T(8,128)(2,1)} %convolution_convert_fusion, bf16[2048,1024]{0,1:T(8,128)(2,1)} %convolution_convert_fusion.1), kind=kLoop, calls=%fused_computation | loop fusion | flops 16777216 | bytes 16777216 | tf_op jit(solution)/shard_map/concatenate | solution.py:135
  89.7 6.0 %multiply_reduce_fusion = bf16[480]{0:T(512)(128)(2,1)S(1)} fusion(f32[480,1024]{1,0:T(8,128)S(1)} %reshape.118, bf16[1,2048,1024]{2,1,0:T(8,128)(2,1)} %param.13, f32[480,2048]{1,0:T(8,128)} %copy-done.3), kind=kOutput, calls=%fused_computation.24 | convolution fusion | flops 2023095808 | bytes 10093504 | tf_op jit(solution)/shard_map/dot_general | solution.py:70
  95.7 0.2 convert_element_type.133
  95.9 5.0 %fusion.19 = bf16[480,1024]{1,0:T(8,128)(2,1)S(1)} fusion(bf16[480,2048]{1,0:T(8,128)(2,1)} %copy-done.4, bf16[1,2048,1024]{2,1,0:T(8,128)(2,1)} %param.12), kind=kOutput, calls=%fused_computation.27 | convolution fusion | flops 2013757440 | bytes 7143424 | tf_op jit(solution)/shard_map/dot_general | solution.py:79
  100.9 0.3 reshape.114
  101.2 0.1 pad_maximum_fusion.2
  101.4 22.5 %all_to_all.11 = bf16[32,15,1025]{2,1,0:T(8,128)(2,1)S(1)} all-to-all(bf16[32,15,1025]{2,1,0:T(8,128)(2,1)S(1)} %pad_maximum_fusion.2), channel_id=1, replica_groups=mesh['expert'=32,'dp'=8] {'expert'}, dimensions={0} | all-to-all | bytes 1968000 | tf_op jit(solution)/shard_map/all_to_all | solution.py:17
  123.9 0.1 split.23
  124.0 1.3 reshape.115
  125.3 0.1 convert_reduce_fusion
  125.5 0.3 select_reduce_fusion.1
  125.8 0.6 pad_maximum_fusion.3
  126.4 2.4 %convolution_convert_fusion.4 = bf16[192,1024]{1,0:T(8,128)(2,1)} fusion(bf16[480,1024]{1,0:T(8,128)(2,1)} %reshape.115, s32[192]{0:T(256)S(1)} %get-tuple-element.28, s32[192]{0:T(256)S(1)} %get-tuple-element.29), kind=kOutput, calls=%fused_computation.28 | convolution fusion | flops 189216768 | bytes 1377792 | tf_op jit(solution)/shard_map/dot_general | solution.py:87
  128.8 56.2 %reduce-scatter.2.cloned.1.call-done = bf16[256,2048]{0,1:T(8,128)(2,1)} async-done(((bf16[2048,2048]{0,1:T(8,128)(2,1)}), bf16[256,2048]{0,1:T(8,128)(2,1)}) %reduce-scatter.2.cloned.1.call-update) | async-done | bytes 1048592 | tf_op jit(solution)/shard_map/reduce_scatter | solution.py:134
  184.9 1.4 convert_element_type.127
  186.3 0.1 slice_bitcast_fusion
  186.5 1.3 copy.32
  187.8 1.3 copy.31
  (25 shorter events, 0.5 us)
Async XLA Ops:
  7.2 6.8 %copy-start = (bf16[192,1024]{1,0:T(8,128)(2,1)S(1)}, bf16[192,1024]{1,0:T(8,128)(2,1)}, u32[]{:S(2)}) copy-start(bf16[192,1024]{1,0:T(8,128)(2,1)} %param.8) | copy-start | bytes 1179652
  7.2 177.7 %reduce-scatter.2.cloned.1.call-start = ((), (), s32[]{:S(2)}) async-start(), calls=%async_computation.3 | async-start | bytes 9437184 | tf_op jit(solution)/shard_map/reduce_scatter | solution.py:134
  63.7 4.6 %copy-start.1 = (bf16[480,1024]{1,0:T(8,128)(2,1)S(1)}, bf16[480,1024]{1,0:T(8,128)(2,1)}, u32[]{:S(2)}) copy-start(bf16[480,1024]{1,0:T(8,128)(2,1)} %convert_element_type.113) | copy-start | bytes 2949124
  63.7 4.6 %copy-start.2 = (bf16[1,2048,1024]{2,1,0:T(8,128)(2,1)S(1)}, bf16[1,2048,1024]{2,1,0:T(8,128)(2,1)}, u32[]{:S(2)}) copy-start(bf16[1,2048,1024]{2,1,0:T(8,128)(2,1)} %param.13) | copy-start | bytes 12582916
  68.3 8.7 %copy-start.3 = (f32[480,2048]{1,0:T(8,128)}, f32[480,2048]{1,0:T(8,128)S(1)}, u32[]{:S(2)}) copy-start(f32[480,2048]{1,0:T(8,128)S(1)} %fusion.2) | copy-start | bytes 11796484
  72.6 4.4 %copy-start.4 = (bf16[480,2048]{1,0:T(8,128)(2,1)}, bf16[480,2048]{1,0:T(8,128)(2,1)S(1)}, u32[]{:S(2)}) copy-start(bf16[480,2048]{1,0:T(8,128)(2,1)S(1)} %fusion.14) | copy-start | bytes 5898244
Sparse Core Ops, SparseCore 0:
  89.8 95.0 reduce-scatter.1
where the time goes:
time: 197 us; the launch traced here: 196 us
  blocking collectives  59 us (30%)
  waiting for transfers between devices  56.2 us (29%)
  matrix products  33 us (17%)
  other arithmetic  19.3 us (10%)
  between operations  14.3 us (7%)
  local copies, waits for them, and re-layouts  14.2 us (7%)
    all_to_all x2, blocking collectives, side_by_side(): lax.all_to_all(both, axis, split_axis=split_dim, concat_axis=concat_dim,...  59 us
    reduce_scatter x1, waiting for transfers between devices, per_device(): lax.psum_scatter(jnp.concatenate([term_in, term_out], axis=1).astype(jnp....  56.2 us
    concatenate x1, other arithmetic, per_device(): jnp.concatenate([term_in, term_out], axis=1).astype(jnp.bfloat16)  8.35 us
    dot_general x1, matrix products, expert_rows(): output = jnp.dot(active_b, weight_out, preferred_element_type=jnp.float32)  6.01 us
    dot_general x1, matrix products, expert_rows(): jnp.dot(hidden_grad, weight_in, preferred_element_type=jnp.float32)  4.98 us
    dot_general x1, matrix products, expert_rows(): lax.dot_general(rows_x, weight_in, (((1,), (1,)), ((), ())), preferred_el...  4.57 us
    dot_general x1, matrix products, per_device(): lax.dot_general(hidden_grad, rows_x, (((0,), (0,)), ((), ())), preferred_...  4.4 us
    dot_general x1, matrix products, per_device(): lax.dot_general(active_b, scaled, (((0,), (0,)), ((), ())), preferred_ele...  4.29 us
  transfers between devices with their start and end apart: 1, of which 1 were waited for; matrix products, arithmetic and copies ran while one was open for 8% of the time, Pallas kernels for 0%

commit v1 on v0

v1 whole, which is shorter than its diff:
```python
import functools

import jax
import jax.numpy as jnp
from jax import lax
from jax.experimental import pallas as pl
from jax.experimental.pallas import tpu as pltpu
from jax.sharding import PartitionSpec as P

MESH = pl.DeviceIdType.MESH
F32, BF16 = jnp.float32, jnp.bfloat16
root_coef = 0.7978845608
cube_coef = 0.044715
SLOT = 16
GATE = 128


def dot(a, b, ca, cb):
    return lax.dot_general(a, b, (((ca,), (cb,)), ((), ())), preferred_element_type=F32)


def gelu_slope(hidden):
    square = hidden * hidden
    tanh_val = jnp.tanh(root_coef * (hidden + cube_coef * square * hidden))
    half = 0.5 * (1.0 + tanh_val)
    slope = half + 0.5 * hidden * (1.0 - tanh_val * tanh_val) * root_coef * (
        1.0 + 3.0 * cube_coef * square
    )
    return hidden * half, slope


def kernel(
    capacity, n_x, n_y,
    tok_hbm, dy_hbm, routes_ref, keep_ref, comb_ref, win_hbm, wout_hbm,
    gtok_ref, gcomb_ref, gin_ref, gout_ref,
    tok, dy, ptok, pdy, meta, pmeta, win, wout,
    sent_x, sent_s, psent_x, psent_s, own_x, own_s, part_x, part_s,
    first_m, second_m, hg_buf, act_buf, tg_acc, gate_acc, back_out, back_in,
    term, got,
    load_sem, pair_send, pair_recv,
    xs, xr, ss, sr, pxs, pxr, pss, psr, bs, br, ring_send, ring_recv,
):
    me = lax.axis_index("expert")
    z = lax.axis_index("dp")
    n_e = n_x * n_y * 2
    n_z = lax.axis_size("dp")
    toks, width = tok.shape
    rows = n_e * SLOT
    core, cx, cy = lax.rem(me, 2), lax.rem(me // 2, n_x), me // (2 * n_x)
    up, down = lax.rem(z + 1, n_z), lax.rem(z + n_z - 1, n_z)
    far = lax.rem(z + n_z // 2, n_z)

    def peer(q):
        cell = lax.rem(q, n_x * n_y)
        dx, dy_ = lax.rem(cell, n_x) + 1, cell // n_x + 1
        dc = 1 - q // (n_x * n_y)
        x, y, c = lax.rem(cx + dx, n_x), lax.rem(cy + dy_, n_y), lax.rem(core + dc, 2)
        return (y * n_x + x) * 2 + c

    loads = [
        pltpu.make_async_copy(src, dst, load_sem.at[k])
        for k, (src, dst) in enumerate(
            ((tok_hbm, tok), (dy_hbm, dy), (win_hbm.at[0], win), (wout_hbm.at[0], wout))
        )
    ]
    for c in loads:
        c.start()

    barrier = pltpu.get_barrier_semaphore()
    for other in (far, up, down):
        pl.semaphore_signal(barrier, inc=1, device_id=(me, other), device_id_type=MESH)

    def greet(q, carry):
        pl.semaphore_signal(barrier, inc=1, device_id=(peer(q), z), device_id_type=MESH)
        return carry

    lax.fori_loop(0, n_e - 1, greet, 0)

    expert_ids = lax.broadcasted_iota(jnp.int32, (n_e, toks), 0)
    r0, r1 = routes_ref[0:1, :], routes_ref[1:2, :]
    keep = keep_ref[...]
    first_hot = jnp.where(r0 == expert_ids, 1.0, 0.0)
    second_hot = jnp.where((r1 == expert_ids) & (keep > 0), 1.0, 0.0)
    earlier = jnp.where(
        lax.broadcasted_iota(jnp.int32, (toks, toks), 0)
        < lax.broadcasted_iota(jnp.int32, (toks, toks), 1), 1.0, 0.0,
    ).astype(BF16)
    first_pos = dot(first_hot.astype(BF16), earlier, 1, 0)
    second_pos = dot(second_hot.astype(BF16), earlier, 1, 0) + jnp.sum(
        first_hot, axis=1, keepdims=True
    )
    first_slot = jnp.sum(first_pos * first_hot, axis=0, keepdims=True)
    second_slot = jnp.sum(second_pos * second_hot, axis=0, keepdims=True)
    first_flat = jnp.where(first_slot < capacity, r0.astype(F32) * SLOT + first_slot, -1.0)
    second_flat = jnp.where(
        (keep > 0) & (second_slot < capacity), r1.astype(F32) * SLOT + second_slot, -1.0
    )
    weight = comb_ref[...].astype(F32)
    meta[0:1, :] = first_flat
    meta[1:2, :] = second_flat
    meta[2:4, :] = weight
    meta[4:8, :] = jnp.zeros((4, toks), F32)
    w0, w1 = weight[0:1, :], weight[1:2, :]
    slot_ids = lax.broadcasted_iota(jnp.int32, (rows, toks), 0).astype(F32)
    hit0, hit1 = slot_ids == first_flat, slot_ids == second_flat
    first_m[...] = jnp.where(hit0, 1.0, 0.0).astype(BF16)
    second_m[...] = jnp.where(hit1, 1.0, 0.0).astype(BF16)
    loads[0].wait()
    sent_x[...] = dot(first_m[...] + second_m[...], tok[...], 1, 0).astype(BF16).reshape(
        n_e, SLOT, width
    )
    weighted = jnp.where(hit0, w0, 0.0) + jnp.where(hit1, w1, 0.0)
    loads[1].wait()
    sent_s[...] = dot(weighted.astype(BF16), dy[...], 1, 0).astype(BF16).reshape(n_e, SLOT, width)

    pl.semaphore_wait(barrier, n_e + 2)

    pair = [
        pltpu.make_async_remote_copy(
            src_ref=src, dst_ref=dst, send_sem=pair_send.at[k], recv_sem=pair_recv.at[k],
            device_id=(me, far), device_id_type=MESH,
        )
        for k, (src, dst) in enumerate(((meta, pmeta), (tok, ptok), (dy, pdy)))
    ]
    for c in pair:
        c.start()

    def hop(src, dst, send, recv, other, slot):
        return pltpu.make_async_remote_copy(
            src_ref=src.at[other], dst_ref=dst.at[slot], send_sem=send.at[other],
            recv_sem=recv.at[slot], device_id=(other, z), device_id_type=MESH,
        )

    def spread(lanes):
        def body(q, carry):
            other = peer(q)
            for src, dst, send, recv in lanes:
                hop(src, dst, send, recv, other, me).start()
            return carry

        lax.fori_loop(0, n_e - 1, body, 0)

    def arrive(lanes):
        def body(q, carry):
            other = lax.rem(me + 1 + q, n_e)
            for src, dst, send, recv in lanes:
                hop(src, dst, send, recv, other, other).wait_recv()
            return carry

        lax.fori_loop(0, n_e - 1, body, 0)

    def drain(lanes):
        def body(q, carry):
            other = lax.rem(me + 1 + q, n_e)
            for src, dst, send, recv in lanes:
                hop(src, dst, send, recv, other, other).wait_send()
            return carry

        lax.fori_loop(0, n_e - 1, body, 0)

    lane_x, lane_s = (sent_x, own_x, xs, xr), (sent_s, own_s, ss, sr)
    lane_px, lane_ps = (psent_x, part_x, pxs, pxr), (psent_s, part_s, pss, psr)
    lane_b = (back_out, back_in, bs, br)
    spread((lane_x, lane_s))
    own_x[me] = sent_x[me]
    own_s[me] = sent_s[me]

    pair[0].wait_recv()
    pair[1].wait_recv()
    p0, p1 = pmeta[0:1, :], pmeta[1:2, :]
    q0, q1 = pmeta[2:3, :], pmeta[3:4, :]
    chosen = jnp.where((slot_ids == p0) | (slot_ids == p1), 1.0, 0.0).astype(BF16)
    psent_x[...] = dot(chosen, ptok[...], 1, 0).astype(BF16).reshape(n_e, SLOT, width)
    spread((lane_px,))
    part_x[me] = psent_x[me]

    half = 128
    ff_dev = gin_ref.shape[0]
    chunks = win.shape[0] // ff_dev
    loads[2].wait()
    loads[3].wait()
    arrive((lane_x, lane_s))
    tg_acc[...] = jnp.zeros_like(tg_acc)
    gate_acc[...] = jnp.zeros_like(gate_acc)

    def own_chunk(c, carry):
        cut = pl.ds(pl.multiple_of(c * ff_dev, ff_dev), ff_dev)
        block = rows // 2
        src = n_e // 2
        for r in range(2):
            x_r = own_x[r * src:(r + 1) * src].reshape(block, width)
            s_r = own_s[r * src:(r + 1) * src].reshape(block, width)
            active, slope = gelu_slope(dot(x_r, win[cut, :], 1, 1))
            active_grad = dot(s_r, wout[cut, :], 1, 1)
            active = active.astype(BF16)
            hidden_grad = (active_grad * slope).astype(BF16)
            piece = pl.ds(r * block, block)
            for k in range(ff_dev // half):
                at = c * (ff_dev // half) + k
                act_buf[at, piece, :] = active[:, k * half:(k + 1) * half]
                hg_buf[at, piece, :] = hidden_grad[:, k * half:(k + 1) * half]
            product = active.astype(F32) * active_grad
            gate_acc[piece, :] += product[:, :half] + product[:, half:]
            tg_acc[piece, :] += dot(hidden_grad, win[cut, :], 1, 0)
        return carry

    lax.fori_loop(0, chunks // 2, own_chunk, 0)

    pair[2].wait_recv()
    weighted = jnp.where(slot_ids == p0, q0, 0.0) + jnp.where(slot_ids == p1, q1, 0.0)
    psent_s[...] = dot(weighted.astype(BF16), pdy[...], 1, 0).astype(BF16).reshape(
        n_e, SLOT, width
    )
    spread((lane_ps,))
    part_s[me] = psent_s[me]

    lax.fori_loop(chunks // 2, chunks, own_chunk, 0)
    back_out[:, :, :width] = tg_acc[...].astype(BF16).reshape(n_e, SLOT, width)
    gate = jnp.sum(gate_acc[...], axis=1, keepdims=True)
    back_out[:, :, width:] = jnp.broadcast_to(gate, (rows, GATE)).astype(BF16).reshape(
        n_e, SLOT, GATE
    )
    spread((lane_b,))
    back_in[me] = back_out[me]

    arrive((lane_px, lane_ps))

    def near(at, store):
        cut = pl.ds(pl.multiple_of(at * half, half), half)
        x_p, s_p = part_x[...].reshape(rows, width), part_s[...].reshape(rows, width)
        active, slope = gelu_slope(dot(x_p, win[cut, :], 1, 1))
        hidden_grad = (dot(s_p, wout[cut, :], 1, 1) * slope).astype(BF16)
        active = active.astype(BF16)
        x_o, s_o = own_x[...].reshape(rows, width), own_s[...].reshape(rows, width)
        store(
            dot(hg_buf[at], x_o, 0, 0) + dot(hidden_grad, x_p, 0, 0),
            dot(act_buf[at], s_o, 0, 0) + dot(active, s_p, 0, 0),
        )

    def ring(k, other):
        return pltpu.make_async_remote_copy(
            src_ref=term.at[k], dst_ref=got.at[k], send_sem=ring_send.at[k],
            recv_sem=ring_recv.at[k], device_id=(me, other), device_id_type=MESH,
        )

    def to_term(k):
        def store(a, b):
            term[k, :, :width] = a.astype(BF16)
            term[k, :, width:] = b.astype(BF16)

        return store

    targets = (
        2 * lax.rem(z + 2, n_z), 2 * lax.rem(z + n_z - 2, n_z) + 1,
        2 * up + 1, 2 * down, 2 * up, 2 * down + 1,
    )
    for k in range(4):
        near(targets[k], to_term(k))
        ring(k, up if k % 2 == 0 else down).start()
    for k in range(4, 6):
        near(targets[k], to_term(k))

    for k in range(2):
        def to_out(a, b, k=k):
            gin_ref[k * half:(k + 1) * half, :] = a
            gout_ref[k * half:(k + 1) * half, :] = b

        near(2 * z + k, to_out)

    for k in range(2):
        ring(k, up if k % 2 == 0 else down).wait_recv()
        term[4 + k] = (term[4 + k].astype(F32) + got[k].astype(F32)).astype(BF16)
        ring(4 + k, up if k % 2 == 0 else down).start()

    arrive((lane_b,))
    back = back_in[...].reshape(rows, width + GATE)
    gtok_ref[...] = dot(first_m[...] + second_m[...], back[:, :width], 0, 0).astype(BF16)
    for k, hits in enumerate((first_m, second_m)):
        grad = dot(back[:, width:], hits[...], 0, 0)
        gcomb_ref[k:k + 1, :] = (grad[0:1, :] / meta[2 + k:3 + k, :]).astype(BF16)

    def gather(k, part):
        piece = slice(part * half, (part + 1) * half)
        gin_ref[piece, :] += got[k, :, :width].astype(F32)
        gout_ref[piece, :] += got[k, :, width:].astype(F32)

    for k, part in ((2, 1), (3, 0), (4, 0), (5, 1)):
        ring(k, up if k % 2 == 0 else down).wait_recv()
        gather(k, part)

    for c in pair:
        c.wait_send()
    drain((lane_x, lane_s, lane_px, lane_ps, lane_b))
    for k in range(6):
        ring(k, up if k % 2 == 0 else down).wait_send()


def per_device(n_x, n_y, tokens, grad_out, routes, keep_second, combine, w_in, w_out):
    n_e = lax.axis_size("expert")
    toks, width = tokens.shape
    ff = w_in.shape[1]
    ff_dev = ff // lax.axis_size("dp")
    capacity = 5 * toks // (2 * n_e)
    rows = n_e * SLOT
    half = 128
    any_spec = pl.BlockSpec(memory_space=pl.ANY)
    vmem_spec = pl.BlockSpec(memory_space=pltpu.VMEM)
    slots = pltpu.VMEM((n_e, SLOT, width), BF16)
    sems = pltpu.SemaphoreType.DMA((n_e,))
    gtok, gcomb, gin, gout = pl.pallas_call(
        functools.partial(kernel, capacity, n_x, n_y),
        out_shape=(
            jax.ShapeDtypeStruct((toks, width), BF16),
            jax.ShapeDtypeStruct((2, toks), BF16),
            jax.ShapeDtypeStruct((ff_dev, width), F32),
            jax.ShapeDtypeStruct((ff_dev, width), F32),
        ),
        in_specs=[any_spec, any_spec, vmem_spec, vmem_spec, vmem_spec, any_spec, any_spec],
        out_specs=(vmem_spec,) * 4,
        scratch_shapes=[pltpu.VMEM((toks, width), BF16)] * 4
        + [pltpu.VMEM((8, toks), F32)] * 2
        + [pltpu.VMEM((ff, width), BF16)] * 2
        + [slots] * 8
        + [pltpu.VMEM((rows, toks), BF16)] * 2
        + [pltpu.VMEM((ff // half, rows, half), BF16)] * 2
        + [pltpu.VMEM((rows, width), F32), pltpu.VMEM((rows, half), F32)]
        + [pltpu.VMEM((n_e, SLOT, width + GATE), BF16)] * 2
        + [pltpu.VMEM((6, half, 2 * width), BF16)] * 2
        + [pltpu.SemaphoreType.DMA((4,)), pltpu.SemaphoreType.DMA((3,)), pltpu.SemaphoreType.DMA((3,))]
        + [sems] * 10
        + [pltpu.SemaphoreType.DMA((6,))] * 2,
        compiler_params=pltpu.CompilerParams(
            collective_id=0, has_side_effects=True, vmem_limit_bytes=60 * 2**20
        ),
    )(
        tokens, grad_out, routes.T, keep_second.reshape(1, toks), combine.T, w_in, w_out,
    )
    return gtok, gcomb.T, gin[None], gout[None]


def solution(mesh):
    n_e = mesh.shape["expert"]
    n_x = 4
    return jax.shard_map(
        functools.partial(per_device, n_x, n_e // (2 * n_x)),
        mesh=mesh,
        in_specs=(
            P(("expert", "dp"), None),
            P(("expert", "dp"), None),
            P(("expert", "dp"), None),
            P(("expert", "dp")),
            P(("expert", "dp"), None),
            P("expert", None, None),
            P("expert", None, None),
        ),
        out_specs=(
            P(("expert", "dp"), None),
            P(("expert", "dp"), None),
            P("expert", "dp", None),
            P("expert", "dp", None),
        ),
        check_vma=False,
    )
```

time: 197 us -> 117 us (0.59)
  Pallas kernels: 0 us -> 108 us
  blocking collectives: 59 us -> 0 us
  waiting for transfers between devices: 56.2 us -> 0 us
  matrix products: 33 us -> 0 us
  other arithmetic: 19.3 us -> 0 us
  between operations: 14.3 us -> 0.64 us
  local copies, waits for them, and re-layouts: 14.2 us -> 7.62 us
    pallas_call x0 -> x1, Pallas kernels: none -> 108 us  [per_device(): pl.pallas_call(functools.partial(kernel, capacity, n_x, n_y), out_shape=(...]
    all_to_all x2 -> x0, blocking collectives: 59 us -> none  [side_by_side(): lax.all_to_all(both, axis, split_axis=split_dim, concat_axis=concat_dim,...]
    reduce_scatter x1 -> x0, waiting for transfers between devices: 56.2 us -> none  [per_device(): lax.psum_scatter(jnp.concatenate([term_in, term_out], axis=1).astype(jnp....]
    dot_general x9 -> x0, matrix products: 33 us -> none  [the longest x1 6.01 us: expert_rows(): output = jnp.dot(active_b, weight_out, preferred_element_type=jnp.float32)]
    concatenate x3 -> x0, other arithmetic: 9.64 us -> none  [the longest x1 8.35 us: per_device(): jnp.concatenate([term_in, term_out], axis=1).astype(jnp.bfloat16)]
    convert_element_type x7 -> x0, local copies, waits for them, and re-layouts: 5.66 us -> none  [the longest x1 2.31 us: expert_rows(): (rows_c.astype(jnp.float32)[:, None] * rows_dy.astype(jnp.float32)).astyp...]
    unnamed x12 -> x4, local copies, waits for them, and re-layouts: 2.64 us -> 7.62 us
    reshape x5 -> x0, local copies, waits for them, and re-layouts: 3.68 us -> none  [the longest x1 1.5 us: per_device(): rows_x = got_x.reshape(sources * capacity, model_width)]
  transfers between devices with their start and end apart: 1 -> 0, of which waited for: 1 -> 0; matrix products, arithmetic and copies ran while one was open for 8% -> 0% of each run, Pallas kernels for 0% -> 0%
where the time goes in v1:
time: 117 us; the launch traced here: 116 us
  Pallas kernels  108 us (92%)
  local copies, waits for them, and re-layouts  7.62 us (7%)
    pallas_call x1, Pallas kernels, per_device(): pl.pallas_call(functools.partial(kernel, capacity, n_x, n_y), out_shape=(...  108 us
    unnamed x4, local copies, waits for them, and re-layouts  7.62 us

profile of v1, /device:TPU:2, one launch (start us, length us, event | category | flops | bytes accessed | tf_op | source)
XLA Modules:
  0.0 116.5 jit_solution(12190801212596425078)
XLA Ops:
  0.6 108.2 %shard_map.102 = (bf16[192,1024]{1,0:T(8,128)(2,1)}, bf16[2,192]{1,0:T(2,128)(2,1)}, f32[256,1024]{1,0:T(8,128)}, f32[256,1024]{1,0:T(8,128)}) custom-call(bf16[192,1024]{1,0:T(8,128)(2,1)} %tok_hbm.1, bf16[192,1024]{1,0:T(8,128)(2,1)} %dy_hbm.1, s32[2,192]{1,0:T(2,128)} %bitcast.8, s32[1,192]{1,0:T(1,128)} %bitcast.9, bf16[2,192]{1,0:T(2,128)(2,1)} %bitcast.10, ...), custom_call_target="tpu_custom_call" | custom-call | tf_op jit(solution)/shard_map/pallas_call | solution.py:310
  108.9 1.8 %copy.15 = bf16[192,1024]{1,0:T(8,128)(2,1)} copy(bf16[192,1024]{1,0:T(8,128)(2,1)} %get-tuple-element.16) | data formatting | bytes 786432
  110.6 1.2 %copy.16 = bf16[192,2]{0,1:T(2,128)(2,1)} copy(bf16[192,2]{0,1:T(2,128)(2,1)} %bitcast.11) | data formatting | bytes 1536
  111.9 2.3 %copy.17 = f32[1,256,1024]{2,1,0:T(8,128)} copy(f32[1,256,1024]{2,1,0:T(8,128)} %bitcast.7) | data formatting | bytes 2097152
  114.2 2.3 %copy.18 = f32[1,256,1024]{2,1,0:T(8,128)} copy(f32[1,256,1024]{2,1,0:T(8,128)} %bitcast.6) | data formatting | bytes 2097152

commit v2 on v1

v2 whole, which is shorter than its diff:
```python
import functools

import jax
import jax.numpy as jnp
from jax import lax
from jax.experimental import pallas as pl
from jax.experimental.pallas import tpu as pltpu
from jax.sharding import PartitionSpec as P

MESH = pl.DeviceIdType.MESH
F32, BF16 = jnp.float32, jnp.bfloat16
root_coef = 0.7978845608
cube_coef = 0.044715
SLOT = 16
GATE = 128
LONG = 64


def dot(a, b, ca, cb):
    return lax.dot_general(a, b, (((ca,), (cb,)), ((), ())), preferred_element_type=F32)


def gelu_slope(hidden):
    square = hidden * hidden
    tanh_val = jnp.tanh(root_coef * (hidden + cube_coef * square * hidden))
    half = 0.5 * (1.0 + tanh_val)
    slope = half + 0.5 * hidden * (1.0 - tanh_val * tanh_val) * root_coef * (
        1.0 + 3.0 * cube_coef * square
    )
    return hidden * half, slope


def kernel(
    capacity, n_x, n_y,
    tok_hbm, dy_hbm, routes_ref, keep_ref, comb_ref, win_hbm, wout_hbm,
    gtok_ref, gcomb_ref, gin_ref, gout_ref,
    tok, dy, ptok, pdy, meta, pmeta, win, wout,
    sent, psent_x, psent_s, own, part_x, part_s,
    first_m, second_m, hg_buf, act_buf, tg_acc, gate_acc, back_out, back_in,
    far_term, far_got, term, got,
    load_sem, pair_send, pair_recv,
    lane_send, lane_recv, ring_send, ring_recv, far_send, far_recv,
):
    me = lax.axis_index("expert")
    z = lax.axis_index("dp")
    n_e = n_x * n_y * 2
    n_z = lax.axis_size("dp")
    toks, width = tok.shape
    rows = n_e * SLOT
    core, cx, cy = lax.rem(me, 2), lax.rem(me // 2, n_x), me // (2 * n_x)
    up, down = lax.rem(z + 1, n_z), lax.rem(z + n_z - 1, n_z)
    far = lax.rem(z + n_z // 2, n_z)

    def peer(q):
        cell = lax.rem(q, n_x * n_y)
        dx, dy_ = lax.rem(cell, n_x) + 1, cell // n_x + 1
        dc = 1 - q // (n_x * n_y)
        x, y, c = lax.rem(cx + dx, n_x), lax.rem(cy + dy_, n_y), lax.rem(core + dc, 2)
        return (y * n_x + x) * 2 + c

    barrier = pltpu.get_barrier_semaphore()
    for other in (far, up, down):
        pl.semaphore_signal(barrier, inc=1, device_id=(me, other), device_id_type=MESH)

    ahead_x = [lax.rem(cx + k, n_x) * 2 for k in range(n_x)]
    ahead_y = [lax.rem(cy + k, n_y) * (2 * n_x) for k in range(n_y)]
    cells = sorted(
        ((dx, dy_) for dx in range(n_x) for dy_ in range(n_y)),
        key=lambda cell: -min(cell[0], n_x - cell[0]) - min(cell[1], n_y - cell[1]),
    )
    for dx, dy_ in cells:
        for c in (core, 1 - core)[0 if dx + dy_ else 1:]:
            pl.semaphore_signal(
                barrier, inc=1, device_id=(ahead_y[dy_] + ahead_x[dx] + c, z), device_id_type=MESH
            )

    loads = [
        pltpu.make_async_copy(src, dst, load_sem.at[k])
        for k, (src, dst) in enumerate(
            ((tok_hbm, tok), (dy_hbm, dy), (win_hbm.at[0], win), (wout_hbm.at[0], wout))
        )
    ]
    for c in loads:
        c.start()

    expert_ids = lax.broadcasted_iota(jnp.int32, (n_e, toks), 0)
    r0, r1 = routes_ref[0:1, :], routes_ref[1:2, :]
    keep = keep_ref[...]
    first_hot = jnp.where(r0 == expert_ids, 1.0, 0.0)
    second_hot = jnp.where((r1 == expert_ids) & (keep > 0), 1.0, 0.0)
    earlier = jnp.where(
        lax.broadcasted_iota(jnp.int32, (toks, toks), 0)
        < lax.broadcasted_iota(jnp.int32, (toks, toks), 1), 1.0, 0.0,
    ).astype(BF16)
    first_pos = dot(first_hot.astype(BF16), earlier, 1, 0)
    second_pos = dot(second_hot.astype(BF16), earlier, 1, 0) + jnp.sum(
        first_hot, axis=1, keepdims=True
    )
    first_slot = jnp.sum(first_pos * first_hot, axis=0, keepdims=True)
    second_slot = jnp.sum(second_pos * second_hot, axis=0, keepdims=True)
    first_flat = jnp.where(first_slot < capacity, r0.astype(F32) * SLOT + first_slot, -1.0)
    second_flat = jnp.where(
        (keep > 0) & (second_slot < capacity), r1.astype(F32) * SLOT + second_slot, -1.0
    )
    weight = comb_ref[...].astype(F32)
    meta[0:1, :] = first_flat
    meta[1:2, :] = second_flat
    meta[2:4, :] = weight
    meta[4:8, :] = jnp.zeros((4, toks), F32)
    w0, w1 = weight[0:1, :], weight[1:2, :]
    slot_ids = lax.broadcasted_iota(jnp.int32, (rows, toks), 0).astype(F32)
    hit0, hit1 = slot_ids == first_flat, slot_ids == second_flat
    first_m[...] = jnp.where(hit0, 1.0, 0.0).astype(BF16)
    second_m[...] = jnp.where(hit1, 1.0, 0.0).astype(BF16)
    loads[0].wait()
    sent[:, 0] = dot(first_m[...] + second_m[...], tok[...], 1, 0).astype(BF16).reshape(
        n_e, SLOT, width
    )
    weighted = jnp.where(hit0, w0, 0.0) + jnp.where(hit1, w1, 0.0)
    loads[1].wait()
    sent[:, 1] = dot(weighted.astype(BF16), dy[...], 1, 0).astype(BF16).reshape(n_e, SLOT, width)

    pl.semaphore_wait(barrier, n_e + 2)

    pair = [
        pltpu.make_async_remote_copy(
            src_ref=src, dst_ref=dst, send_sem=pair_send.at[k], recv_sem=pair_recv.at[k],
            device_id=(me, far), device_id_type=MESH,
        )
        for k, (src, dst) in enumerate(((meta, pmeta), (tok, ptok), (dy, pdy)))
    ]
    for c in pair:
        c.start()

    lanes = ((sent, own), (psent_x, part_x), (psent_s, part_s), (back_out, back_in))

    def hop(lane, src, dst, other):
        return pltpu.make_async_remote_copy(
            src_ref=lanes[lane][0].at[src], dst_ref=lanes[lane][1].at[dst],
            send_sem=lane_send.at[lane], recv_sem=lane_recv.at[lane],
            device_id=(other, z), device_id_type=MESH,
        )

    def spread(lane):
        def body(q, carry):
            other = peer(q)
            hop(lane, other, me, other).start()
            return carry

        lax.fori_loop(0, n_e - 1, body, 0)
        lanes[lane][1][me] = lanes[lane][0][me]

    def whole(lane):
        return hop(lane, pl.ds(0, n_e - 1), pl.ds(0, n_e - 1), lax.rem(me + 1, n_e))

    spread(0)

    pair[0].wait_recv()
    pair[1].wait_recv()
    p0, p1 = pmeta[0:1, :], pmeta[1:2, :]
    q0, q1 = pmeta[2:3, :], pmeta[3:4, :]
    chosen = jnp.where((slot_ids == p0) | (slot_ids == p1), 1.0, 0.0).astype(BF16)
    psent_x[...] = dot(chosen, ptok[...], 1, 0).astype(BF16).reshape(n_e, SLOT, width)
    spread(1)

    ff_dev = gin_ref.shape[0]
    near_rows = ff_dev - LONG
    chunks = win.shape[0] // ff_dev
    loads[2].wait()
    loads[3].wait()
    whole(0).wait_recv()
    tg_acc[...] = jnp.zeros_like(tg_acc)
    gate_acc[...] = jnp.zeros_like(gate_acc)
    block, src = rows // 2, n_e // 2

    def own_chunk(j, carry):
        odd = lax.rem(j, 2)
        target = lax.rem(z + n_z // 2 + (1 - odd) * (j // 2) - odd * ((j + 1) // 2), n_z)
        cut = pl.ds(pl.multiple_of(target * ff_dev, ff_dev), ff_dev)
        for r in range(2):
            x_r = own[r * src:(r + 1) * src, 0].reshape(block, width)
            s_r = own[r * src:(r + 1) * src, 1].reshape(block, width)
            active, slope = gelu_slope(dot(x_r, win[cut, :], 1, 1))
            active_grad = dot(s_r, wout[cut, :], 1, 1)
            active = active.astype(BF16)
            hidden_grad = (active_grad * slope).astype(BF16)
            piece = pl.ds(r * block, block)
            act_buf[target, piece, :] = active
            hg_buf[target, piece, :] = hidden_grad
            product = active.astype(F32) * active_grad
            gate_acc[piece, :] += product[:, :GATE] + product[:, GATE:]
            tg_acc[piece, :] += dot(hidden_grad, win[cut, :], 1, 0)
        for m, left in enumerate((hg_buf, act_buf)):
            part = dot(
                left[target, :, ff_dev - 128:], own[:, m].reshape(rows, width), 0, 0
            )
            far_term[j, m] = part[128 - LONG:].astype(BF16)
        return carry

    def own_chunks(start, stop):
        lax.fori_loop(start, stop, own_chunk, 0)

    long_up = ((0, 0), (1, 1), (1, 0), (3, 1), (3, 0), (5, 1), (5, 0))
    long_down = ((0, 1), (2, 0), (2, 1), (4, 0), (4, 1), (6, 0), (6, 1))

    def long_hop(side, k):
        j, m = (long_up, long_down)[side][k]
        return pltpu.make_async_remote_copy(
            src_ref=far_term.at[j, m], dst_ref=far_got.at[side, k],
            send_sem=far_send.at[side, k], recv_sem=far_recv.at[side, k],
            device_id=(me, (up, down)[side]), device_id_type=MESH,
        )

    def relay(k):
        for side in range(2):
            j, m = (long_up, long_down)[side][k + 2]
            long_hop(side, k).wait_recv()
            far_term[j, m] = (far_term[j, m].astype(F32) + far_got[side, k].astype(F32)).astype(BF16)
            long_hop(side, k + 2).start()

    own_chunks(0, 3)
    for k in range(2):
        for side in range(2):
            long_hop(side, k).start()
    own_chunks(3, 4)

    pair[2].wait_recv()
    weighted = jnp.where(slot_ids == p0, q0, 0.0) + jnp.where(slot_ids == p1, q1, 0.0)
    psent_s[...] = dot(weighted.astype(BF16), pdy[...], 1, 0).astype(BF16).reshape(
        n_e, SLOT, width
    )
    spread(2)

    own_chunks(4, 5)
    relay(0)
    own_chunks(5, 6)
    relay(1)
    own_chunks(6, 8)
    relay(2)
    back_out[:, :, :width] = tg_acc[...].astype(BF16).reshape(n_e, SLOT, width)
    gate = jnp.sum(gate_acc[...], axis=1, keepdims=True)
    back_out[:, :, width:] = jnp.broadcast_to(gate, (rows, GATE)).astype(BF16).reshape(
        n_e, SLOT, GATE
    )
    relay(3)
    whole(1).wait_recv()
    whole(2).wait_recv()
    def near(target, store_in, store_out):
        cut = pl.ds(pl.multiple_of(target * ff_dev, ff_dev), ff_dev)
        x_p, s_p = part_x[...].reshape(rows, width), part_s[...].reshape(rows, width)
        x_o, s_o = own[:, 0].reshape(rows, width), own[:, 1].reshape(rows, width)
        active, slope = gelu_slope(dot(x_p, win[cut, :], 1, 1))
        if store_in:
            hidden_grad = (dot(s_p, wout[cut, :], 1, 1) * slope).astype(BF16)
            grad = dot(hg_buf[target], x_o, 0, 0) + dot(hidden_grad, x_p, 0, 0)
            store_in(grad[:near_rows])
        if store_out:
            grad = dot(act_buf[target], s_o, 0, 0) + dot(active.astype(BF16), s_p, 0, 0)
            store_out(grad[:near_rows])

    def ring(k):
        return pltpu.make_async_remote_copy(
            src_ref=term.at[k], dst_ref=got.at[k], send_sem=ring_send.at[k],
            recv_sem=ring_recv.at[k], device_id=(me, down if k % 2 else up), device_id_type=MESH,
        )

    def to_term(k):
        def store(grad):
            term[k] = grad.astype(BF16)

        return store

    def to_out(ref):
        def store(grad):
            ref[:near_rows, :] = grad

        return store

    near(lax.rem(z + 2, n_z), to_term(0), None)
    ring(0).start()
    near(lax.rem(z + n_z - 2, n_z), None, to_term(1))
    ring(1).start()
    relay(4)
    spread(3)
    near(up, to_term(4), to_term(2))
    ring(2).start()
    near(down, to_term(3), to_term(5))
    ring(3).start()
    near(z, to_out(gin_ref), to_out(gout_ref))
    for m, (ref, k_up, k_down) in enumerate(((gin_ref, 6, 5), (gout_ref, 5, 6))):
        long_hop(0, k_up).wait_recv()
        long_hop(1, k_down).wait_recv()
        ref[near_rows:, :] = (
            far_term[chunks - 1, m].astype(F32)
            + far_got[0, k_up].astype(F32) + far_got[1, k_down].astype(F32)
        )
    for k in range(2):
        ring(k).wait_recv()
        term[4 + k] = (term[4 + k].astype(F32) + got[k].astype(F32)).astype(BF16)
        ring(4 + k).start()

    whole(3).wait_recv()
    back = back_in[...].reshape(rows, width + GATE)
    gtok_ref[...] = dot(first_m[...] + second_m[...], back[:, :width], 0, 0).astype(BF16)
    for k, hits in enumerate((first_m, second_m)):
        grad = dot(back[:, width:], hits[...], 0, 0)
        gcomb_ref[k:k + 1, :] = (grad[0:1, :] / meta[2 + k:3 + k, :]).astype(BF16)

    for k, ref in ((2, gout_ref), (3, gin_ref), (4, gin_ref), (5, gout_ref)):
        ring(k).wait_recv()
        ref[:near_rows, :] += got[k].astype(F32)

    for c in pair:
        c.wait_send()
    for lane in range(len(lanes)):
        whole(lane).wait_send()
    for k in range(6):
        ring(k).wait_send()
    for side in range(2):
        for k in range(len(long_up)):
            long_hop(side, k).wait_send()


def hand_out(*refs):
    copies = [pltpu.make_async_copy(refs[k], refs[4 + k], refs[8].at[k]) for k in range(4)]
    for c in copies:
        c.start()
    for c in copies:
        c.wait()


def per_device(n_x, n_y, tokens, grad_out, routes, keep_second, combine, w_in, w_out):
    n_e = lax.axis_size("expert")
    toks, width = tokens.shape
    ff = w_in.shape[1]
    ff_dev = ff // lax.axis_size("dp")
    capacity = 5 * toks // (2 * n_e)
    rows = n_e * SLOT
    any_spec = pl.BlockSpec(memory_space=pltpu.HBM)
    vmem_spec = pl.BlockSpec(memory_space=pltpu.VMEM)
    slots = pltpu.VMEM((n_e, SLOT, width), BF16)
    pairs = pltpu.VMEM((n_e, 2, SLOT, width), BF16)
    results = pl.pallas_call(
        functools.partial(kernel, capacity, n_x, n_y),
        out_shape=(
            pltpu.VMEM((toks, width), BF16),
            pltpu.VMEM((2, toks), BF16),
            pltpu.VMEM((ff_dev, width), F32),
            pltpu.VMEM((ff_dev, width), F32),
        ),
        in_specs=[any_spec, any_spec, vmem_spec, vmem_spec, vmem_spec, any_spec, any_spec],
        out_specs=(vmem_spec,) * 4,
        scratch_shapes=[pltpu.VMEM((toks, width), BF16)] * 4
        + [pltpu.VMEM((8, toks), F32)] * 2
        + [pltpu.VMEM((ff, width), BF16)] * 2
        + [pairs, slots, slots, pairs, slots, slots]
        + [pltpu.VMEM((rows, toks), BF16)] * 2
        + [pltpu.VMEM((ff // ff_dev, rows, ff_dev), BF16)] * 2
        + [pltpu.VMEM((rows, width), F32), pltpu.VMEM((rows, GATE), F32)]
        + [pltpu.VMEM((n_e, SLOT, width + GATE), BF16)] * 2
        + [pltpu.VMEM((ff // ff_dev, 2, LONG, width), BF16), pltpu.VMEM((2, 7, LONG, width), BF16)]
        + [pltpu.VMEM((6, ff_dev - LONG, width), BF16)] * 2
        + [pltpu.SemaphoreType.DMA((4,)), pltpu.SemaphoreType.DMA((3,)), pltpu.SemaphoreType.DMA((3,))]
        + [pltpu.SemaphoreType.DMA((4,))] * 2
        + [pltpu.SemaphoreType.DMA((6,))] * 2
        + [pltpu.SemaphoreType.DMA((2, 7))] * 2,
        compiler_params=pltpu.CompilerParams(
            collective_id=0, has_side_effects=True, vmem_limit_bytes=58 * 2**20
        ),
    )(
        tokens, grad_out, routes.T, keep_second.reshape(1, toks), combine.T, w_in, w_out,
    )
    gtok, gcomb, gin, gout = pl.pallas_call(
        hand_out,
        out_shape=tuple(jax.ShapeDtypeStruct(r.shape, r.dtype) for r in results),
        in_specs=[vmem_spec] * 4,
        out_specs=(any_spec,) * 4,
        scratch_shapes=[pltpu.SemaphoreType.DMA((4,))],
        compiler_params=pltpu.CompilerParams(vmem_limit_bytes=8 * 2**20),
    )(*results)
    return gtok, gcomb.T, gin[None], gout[None]


def solution(mesh):
    n_e = mesh.shape["expert"]
    n_x = 4
    return jax.shard_map(
        functools.partial(per_device, n_x, n_e // (2 * n_x)),
        mesh=mesh,
        in_specs=(
            P(("expert", "dp"), None),
            P(("expert", "dp"), None),
            P(("expert", "dp"), None),
            P(("expert", "dp")),
            P(("expert", "dp"), None),
            P("expert", None, None),
            P("expert", None, None),
        ),
        out_specs=(
            P(("expert", "dp"), None),
            P(("expert", "dp"), None),
            P("expert", "dp", None),
            P("expert", "dp", None),
        ),
        check_vma=False,
    )
```

time: 117 us -> 98.4 us (0.84)
  Pallas kernels: 108 us -> 96.8 us
  local copies, waits for them, and re-layouts: 7.62 us -> 0 us
    pallas_call x1, Pallas kernels: 108 us -> 95.3 us  [per_device(): pl.pallas_call(functools.partial(kernel, capacity, n_x, n_y), out_shape=(...]
    unnamed x4 -> x0, local copies, waits for them, and re-layouts: 7.62 us -> none
    pallas_call x0 -> x1, Pallas kernels: none -> 1.49 us  [per_device(): pl.pallas_call(hand_out, out_shape=tuple((jax.ShapeDtypeStruct(r.shape, r...]
where the time goes in v2:
time: 98.4 us; the launch traced here: 97.6 us
  Pallas kernels  96.8 us (98%)
    pallas_call x1, Pallas kernels, per_device(): pl.pallas_call(functools.partial(kernel, capacity, n_x, n_y), out_shape=(...  95.3 us

profile of v2, /device:TPU:2, one launch (start us, length us, event | category | flops | bytes accessed | tf_op | source)
XLA Modules:
  0.0 97.6 jit_solution(15563454881984744075)
XLA Ops:
  0.6 95.3 %shard_map.102 = (bf16[192,1024]{1,0:T(8,128)(2,1)S(1)}, bf16[2,192]{1,0:T(2,128)(2,1)S(1)}, f32[256,1024]{1,0:T(8,128)S(1)}, f32[256,1024]{1,0:T(8,128)S(1)}) custom-call(bf16[192,1024]{1,0:T(8,128)(2,1)} %tok_hbm.1, bf16[192,1024]{1,0:T(8,128)(2,1)} %dy_hbm.1, s32[2,192]{1,0:T(2,128)} %bitcast.6, s32[1,192]{1,0:T(1,128)} %bitcast.7, ...), custom_call_target="tpu_custom_call" | custom-call | tf_op jit(solution)/shard_map/pallas_call | solution.py:343
  96.0 1.5 %shard_map.103 = (bf16[192,1024]{1,0:T(8,128)(2,1)}, bf16[2,192]{1,0:T(2,128)(2,1)}, f32[256,1024]{1,0:T(8,128)}, f32[256,1024]{1,0:T(8,128)}) custom-call(bf16[192,1024]{1,0:T(8,128)(2,1)S(1)} %get-tuple-element.12.refs_0_, bf16[2,192]{1,0:T(2,128)(2,1)S(1)} %get-tuple-element.13.refs_1_, f32[256,1024]{1,0:T(8,128)S(1)} %get-tuple-element.14.refs_2_, ...), custom_call_target="tpu_custom_call" | custom-call | tf_op jit(solution)/shard_map/pallas_call | solution.py:373

commit v3 on v2

--- a/solution.py
+++ b/solution.py
@@ -13,7 +13,8 @@
 cube_coef = 0.044715
 SLOT = 16
 GATE = 128
-LONG = 64
+PARTS = 2
+LONG = 48
 
 
 def dot(a, b, ca, cb):
@@ -32,12 +33,12 @@
 
 def kernel(
     capacity, n_x, n_y,
-    tok_hbm, dy_hbm, routes_ref, keep_ref, comb_ref, win_hbm, wout_hbm,
+    tok_hbm, dy_hbm, routes_hbm, keep_hbm, comb_hbm, win_hbm, wout_hbm,
     gtok_ref, gcomb_ref, gin_ref, gout_ref,
-    tok, dy, ptok, pdy, meta, pmeta, win, wout,
+    routes_ref, keep_ref, comb_ref, tok, dy, ptok, pdy, meta, pmeta, win, wout,
     sent, psent_x, psent_s, own, part_x, part_s,
-    first_m, second_m, hg_buf, act_buf, tg_acc, gate_acc, back_out, back_in,
-    far_term, far_got, term, got,
+    first_m, second_m, chosen_m, weighted_m, hg_buf, act_buf, tg_acc, gate_acc, back_out, back_in,
+    far_term, far_got, slope_pre, act_pre, term, got,
     load_sem, pair_send, pair_recv,
     lane_send, lane_recv, ring_send, ring_recv, far_send, far_recv,
 ):
@@ -51,13 +52,6 @@
     up, down = lax.rem(z + 1, n_z), lax.rem(z + n_z - 1, n_z)
     far = lax.rem(z + n_z // 2, n_z)
 
-    def peer(q):
-        cell = lax.rem(q, n_x * n_y)
-        dx, dy_ = lax.rem(cell, n_x) + 1, cell // n_x + 1
-        dc = 1 - q // (n_x * n_y)
-        x, y, c = lax.rem(cx + dx, n_x), lax.rem(cy + dy_, n_y), lax.rem(core + dc, 2)
-        return (y * n_x + x) * 2 + c
-
     barrier = pltpu.get_barrier_semaphore()
     for other in (far, up, down):
         pl.semaphore_signal(barrier, inc=1, device_id=(me, other), device_id_type=MESH)
@@ -68,21 +62,27 @@
         ((dx, dy_) for dx in range(n_x) for dy_ in range(n_y)),
         key=lambda cell: -min(cell[0], n_x - cell[0]) - min(cell[1], n_y - cell[1]),
     )
-    for dx, dy_ in cells:
-        for c in (core, 1 - core)[0 if dx + dy_ else 1:]:
-            pl.semaphore_signal(
-                barrier, inc=1, device_id=(ahead_y[dy_] + ahead_x[dx] + c, z), device_id_type=MESH
-            )
+    peers = [
+        ahead_y[dy_] + ahead_x[dx] + c
+        for c in (1 - core, core) for dx, dy_ in cells
+    ][:-1]
+    for other in peers:
+        pl.semaphore_signal(barrier, inc=1, device_id=(other, z), device_id_type=MESH)
 
     loads = [
         pltpu.make_async_copy(src, dst, load_sem.at[k])
         for k, (src, dst) in enumerate(
-            ((tok_hbm, tok), (dy_hbm, dy), (win_hbm.at[0], win), (wout_hbm.at[0], wout))
+            (
+                (tok_hbm, tok), (dy_hbm, dy), (win_hbm.at[0], win), (wout_hbm.at[0], wout),
+                (routes_hbm, routes_ref), (keep_hbm, keep_ref), (comb_hbm, comb_ref),
+            )
         )
     ]
-    for c in loads:
-        c.start()
-
+    for k in (4, 5, 6, 0, 1, 2, 3):
+        loads[k].start()
+
+    for k in (4, 5, 6):
+        loads[k].wait()
     expert_ids = lax.broadcasted_iota(jnp.int32, (n_e, toks), 0)
     r0, r1 = routes_ref[0:1, :], routes_ref[1:2, :]
     keep = keep_ref[...]
@@ -122,46 +122,67 @@
 
     pl.semaphore_wait(barrier, n_e + 2)
 
+    cuts = [pl.ds(k * (width // PARTS), width // PARTS) for k in range(PARTS)]
     pair = [
         pltpu.make_async_remote_copy(
             src_ref=src, dst_ref=dst, send_sem=pair_send.at[k], recv_sem=pair_recv.at[k],
             device_id=(me, far), device_id_type=MESH,
         )
-        for k, (src, dst) in enumerate(((meta, pmeta), (tok, ptok), (dy, pdy)))
+        for k, (src, dst) in enumerate(
+            [(meta, pmeta)]
+            + [(src.at[:, cut], dst.at[:, cut]) for src, dst in ((tok, ptok), (dy, pdy)) for cut in cuts]
+        )
     ]
     for c in pair:
         c.start()
 
-    lanes = ((sent, own), (psent_x, part_x), (psent_s, part_s), (back_out, back_in))
-
-    def hop(lane, src, dst, other):
+    lanes = ((sent, own), (back_out, back_in), (psent_x, part_x), (psent_s, part_s))
+    last = len(lanes) - 2
+
+    def hop(lane, src, dst, other, part=None):
+        (left, right), sem = lanes[lane], lane
+        left, right = left.at[src], right.at[dst]
+        if part is not None:
+            tail = (slice(None),) * (len(left.shape) - 1) + (cuts[part],)
+            left, right = left.at[tail], right.at[tail]
+            sem = last + (lane - last) * PARTS + part
         return pltpu.make_async_remote_copy(
-            src_ref=lanes[lane][0].at[src], dst_ref=lanes[lane][1].at[dst],
-            send_sem=lane_send.at[lane], recv_sem=lane_recv.at[lane],
+            src_ref=left, dst_ref=right, send_sem=lane_send.at[sem], recv_sem=lane_recv.at[sem],
             device_id=(other, z), device_id_type=MESH,
         )
 
-    def spread(lane):
-        def body(q, carry):
-            other = peer(q)
-            hop(lane, other, me, other).start()
-            return carry
-
-        lax.fori_loop(0, n_e - 1, body, 0)
-        lanes[lane][1][me] = lanes[lane][0][me]
-
-    def whole(lane):
-        return hop(lane, pl.ds(0, n_e - 1), pl.ds(0, n_e - 1), lax.rem(me + 1, n_e))
+    def spread(lane, part=None):
+        for other in peers:
+            hop(lane, other, me, other, part).start()
+        left, right = lanes[lane]
+        if part is None:
+            right[me] = left[me]
+        else:
+            right[me, :, cuts[part]] = left[me, :, cuts[part]]
+
+    def whole(lane, part=None):
+        return hop(lane, pl.ds(0, n_e - 1), pl.ds(0, n_e - 1), lax.rem(me + 1, n_e), part)
 
     spread(0)
 
     pair[0].wait_recv()
-    pair[1].wait_recv()
     p0, p1 = pmeta[0:1, :], pmeta[1:2, :]
     q0, q1 = pmeta[2:3, :], pmeta[3:4, :]
-    chosen = jnp.where((slot_ids == p0) | (slot_ids == p1), 1.0, 0.0).astype(BF16)
-    psent_x[...] = dot(chosen, ptok[...], 1, 0).astype(BF16).reshape(n_e, SLOT, width)
-    spread(1)
+    chosen_m[...] = jnp.where((slot_ids == p0) | (slot_ids == p1), 1.0, 0.0).astype(BF16)
+    weighted_m[...] = (
+        jnp.where(slot_ids == p0, q0, 0.0) + jnp.where(slot_ids == p1, q1, 0.0)
+    ).astype(BF16)
+
+    def forward(lane, part):
+        pair[1 + (lane - last) * PARTS + part].wait_recv()
+        picks, source, out = ((chosen_m, ptok, psent_x), (weighted_m, pdy, psent_s))[lane - last]
+        out[:, :, cuts[part]] = dot(picks[...], source[:, cuts[part]], 1, 0).astype(BF16).reshape(
+            n_e, SLOT, width // PARTS
+        )
+        spread(lane, part)
+
+    for part in range(PARTS):
+        forward(2, part)
 
     ff_dev = gin_ref.shape[0]
     near_rows = ff_dev - LONG
@@ -223,40 +244,52 @@
         for side in range(2):
             long_hop(side, k).start()
     own_chunks(3, 4)
-
-    pair[2].wait_recv()
-    weighted = jnp.where(slot_ids == p0, q0, 0.0) + jnp.where(slot_ids == p1, q1, 0.0)
-    psent_s[...] = dot(weighted.astype(BF16), pdy[...], 1, 0).astype(BF16).reshape(
-        n_e, SLOT, width
-    )
-    spread(2)
-
+    forward(3, 0)
     own_chunks(4, 5)
+    for part in range(1, PARTS):
+        forward(3, part)
+
+    own_chunks(5, 6)
     relay(0)
-    own_chunks(5, 6)
+    own_chunks(6, 7)
     relay(1)
-    own_chunks(6, 8)
+    own_chunks(7, 8)
     relay(2)
     back_out[:, :, :width] = tg_acc[...].astype(BF16).reshape(n_e, SLOT, width)
     gate = jnp.sum(gate_acc[...], axis=1, keepdims=True)
     back_out[:, :, width:] = jnp.broadcast_to(gate, (rows, GATE)).astype(BF16).reshape(
         n_e, SLOT, GATE
     )
+    for part in range(PARTS):
+        whole(2, part).wait_recv()
+    above, below = lax.rem(z + 2, n_z), lax.rem(z + n_z - 2, n_z)
+
+    def units(target):
+        return pl.ds(pl.multiple_of(target * ff_dev, ff_dev), ff_dev)
+
+    def rows_of(array):
+        return array.reshape(rows, width)
+
+    active, slope = gelu_slope(dot(rows_of(part_x[...]), win[units(above), :], 1, 1))
+    slope_pre[...] = slope
+    active, slope = gelu_slope(dot(rows_of(part_x[...]), win[units(below), :], 1, 1))
+    act_pre[...] = active.astype(BF16)
     relay(3)
-    whole(1).wait_recv()
-    whole(2).wait_recv()
+    gin_ref[...] = dot(hg_buf[above], rows_of(own[:, 0]), 0, 0)
+    gout_ref[...] = dot(act_buf[below], rows_of(own[:, 1]), 0, 0)
+    relay(4)
+    for part in range(PARTS):
+        whole(3, part).wait_recv()
+
     def near(target, store_in, store_out):
-        cut = pl.ds(pl.multiple_of(target * ff_dev, ff_dev), ff_dev)
-        x_p, s_p = part_x[...].reshape(rows, width), part_s[...].reshape(rows, width)
-        x_o, s_o = own[:, 0].reshape(rows, width), own[:, 1].reshape(rows, width)
-        active, slope = gelu_slope(dot(x_p, win[cut, :], 1, 1))
-        if store_in:
-            hidden_grad = (dot(s_p, wout[cut, :], 1, 1) * slope).astype(BF16)
-            grad = dot(hg_buf[target], x_o, 0, 0) + dot(hidden_grad, x_p, 0, 0)
-            store_in(grad[:near_rows])
-        if store_out:
-            grad = dot(act_buf[target], s_o, 0, 0) + dot(active.astype(BF16), s_p, 0, 0)
-            store_out(grad[:near_rows])
+        x_p, s_p = rows_of(part_x[...]), rows_of(part_s[...])
+        x_o, s_o = rows_of(own[:, 0]), rows_of(own[:, 1])
+        active, slope = gelu_slope(dot(x_p, win[units(target), :], 1, 1))
+        hidden_grad = (dot(s_p, wout[units(target), :], 1, 1) * slope).astype(BF16)
+        grad = dot(hg_buf[target], x_o, 0, 0) + dot(hidden_grad, x_p, 0, 0)
+        store_in(grad[:near_rows])
+        grad = dot(act_buf[target], s_o, 0, 0) + dot(active.astype(BF16), s_p, 0, 0)
+        store_out(grad[:near_rows])
 
     def ring(k):
         return pltpu.make_async_remote_copy(
@@ -276,12 +309,16 @@
 
         return store
 
-    near(lax.rem(z + 2, n_z), to_term(0), None)
+    grad = gout_ref[...] + dot(act_pre[...], rows_of(part_s[...]), 0, 0)
+    to_term(1)(grad[:near_rows])
+    ring(1).start()
+    hidden_grad = (
+        dot(rows_of(part_s[...]), wout[units(above), :], 1, 1) * slope_pre[...]
+    ).astype(BF16)
+    grad = gin_ref[...] + dot(hidden_grad, rows_of(part_x[...]), 0, 0)
+    to_term(0)(grad[:near_rows])
     ring(0).start()
-    near(lax.rem(z + n_z - 2, n_z), None, to_term(1))
-    ring(1).start()
-    relay(4)
-    spread(3)
+    spread(1)
     near(up, to_term(4), to_term(2))
     ring(2).start()
     near(down, to_term(3), to_term(5))
@@ -299,7 +336,7 @@
         term[4 + k] = (term[4 + k].astype(F32) + got[k].astype(F32)).astype(BF16)
         ring(4 + k).start()
 
-    whole(3).wait_recv()
+    whole(1).wait_recv()
     back = back_in[...].reshape(rows, width + GATE)
     gtok_ref[...] = dot(first_m[...] + second_m[...], back[:, :width], 0, 0).astype(BF16)
     for k, hits in enumerate((first_m, second_m)):
@@ -312,8 +349,11 @@
 
     for c in pair:
         c.wait_send()
-    for lane in range(len(lanes)):
+    for lane in range(last):
         whole(lane).wait_send()
+    for lane in range(last, len(lanes)):
+        for part in range(PARTS):
+            whole(lane, part).wait_send()
     for k in range(6):
         ring(k).wait_send()
     for side in range(2):
@@ -348,20 +388,24 @@
             pltpu.VMEM((ff_dev, width), F32),
             pltpu.VMEM((ff_dev, width), F32),
         ),
-        in_specs=[any_spec, any_spec, vmem_spec, vmem_spec, vmem_spec, any_spec, any_spec],
+        in_specs=[any_spec] * 7,
         out_specs=(vmem_spec,) * 4,
-        scratch_shapes=[pltpu.VMEM((toks, width), BF16)] * 4
+        scratch_shapes=[pltpu.VMEM((2, toks), jnp.int32), pltpu.VMEM((1, toks), jnp.int32)]
+        + [pltpu.VMEM((2, toks), BF16)]
+        + [pltpu.VMEM((toks, width), BF16)] * 4
         + [pltpu.VMEM((8, toks), F32)] * 2
         + [pltpu.VMEM((ff, width), BF16)] * 2
         + [pairs, slots, slots, pairs, slots, slots]
-        + [pltpu.VMEM((rows, toks), BF16)] * 2
+        + [pltpu.VMEM((rows, toks), BF16)] * 4
         + [pltpu.VMEM((ff // ff_dev, rows, ff_dev), BF16)] * 2
         + [pltpu.VMEM((rows, width), F32), pltpu.VMEM((rows, GATE), F32)]
         + [pltpu.VMEM((n_e, SLOT, width + GATE), BF16)] * 2
         + [pltpu.VMEM((ff // ff_dev, 2, LONG, width), BF16), pltpu.VMEM((2, 7, LONG, width), BF16)]
+        + [pltpu.VMEM((rows, ff_dev), F32), pltpu.VMEM((rows, ff_dev), BF16)]
         + [pltpu.VMEM((6, ff_dev - LONG, width), BF16)] * 2
-        + [pltpu.SemaphoreType.DMA((4,)), pltpu.SemaphoreType.DMA((3,)), pltpu.SemaphoreType.DMA((3,))]
-        + [pltpu.SemaphoreType.DMA((4,))] * 2
+        + [pltpu.SemaphoreType.DMA((7,))]
+        + [pltpu.SemaphoreType.DMA((1 + 2 * PARTS,))] * 2
+        + [pltpu.SemaphoreType.DMA((2 + 2 * PARTS,))] * 2
         + [pltpu.SemaphoreType.DMA((6,))] * 2
         + [pltpu.SemaphoreType.DMA((2, 7))] * 2,
         compiler_params=pltpu.CompilerParams(

time: 98.4 us -> 94.6 us (0.961)
  Pallas kernels: 96.8 us -> 93.6 us
    pallas_call x1, Pallas kernels: 95.3 us -> 92.2 us  [per_device(): pl.pallas_call(functools.partial(kernel, capacity, n_x, n_y), out_shape=(...]
where the time goes in v3:
time: 94.6 us; the launch traced here: 94.5 us
  Pallas kernels  93.6 us (99%)
    pallas_call x1, Pallas kernels, per_device(): pl.pallas_call(functools.partial(kernel, capacity, n_x, n_y), out_shape=(...  92.2 us

profile of v3, /device:TPU:2, one launch (start us, length us, event | category | flops | bytes accessed | tf_op | source)
XLA Modules:
  0.0 94.5 jit_solution(14863959711769327829)
XLA Ops:
  0.6 92.2 %shard_map.102 = (bf16[192,1024]{1,0:T(8,128)(2,1)S(1)}, bf16[2,192]{1,0:T(2,128)(2,1)S(1)}, f32[256,1024]{1,0:T(8,128)S(1)}, f32[256,1024]{1,0:T(8,128)S(1)}) custom-call(bf16[192,1024]{1,0:T(8,128)(2,1)} %tok_hbm.1, bf16[192,1024]{1,0:T(8,128)(2,1)} %dy_hbm.1, s32[2,192]{1,0:T(2,128)} %bitcast.6, s32[1,192]{1,0:T(1,128)} %bitcast.7, ...), custom_call_target="tpu_custom_call" | custom-call | tf_op jit(solution)/shard_map/pallas_call | solution.py:383
  92.8 1.5 %shard_map.103 = (bf16[192,1024]{1,0:T(8,128)(2,1)}, bf16[2,192]{1,0:T(2,128)(2,1)}, f32[256,1024]{1,0:T(8,128)}, f32[256,1024]{1,0:T(8,128)}) custom-call(bf16[192,1024]{1,0:T(8,128)(2,1)S(1)} %get-tuple-element.12.refs_0_, bf16[2,192]{1,0:T(2,128)(2,1)S(1)} %get-tuple-element.13.refs_1_, f32[256,1024]{1,0:T(8,128)S(1)} %get-tuple-element.14.refs_2_, ...), custom_call_target="tpu_custom_call" | custom-call | tf_op jit(solution)/shard_map/pallas_call | solution.py:417

commit v4 on v3

--- a/solution.py
+++ b/solution.py
@@ -14,7 +14,7 @@
 SLOT = 16
 GATE = 128
 PARTS = 2
-LONG = 48
+LONG = 32
 
 
 def dot(a, b, ca, cb):
@@ -38,7 +38,7 @@
     routes_ref, keep_ref, comb_ref, tok, dy, ptok, pdy, meta, pmeta, win, wout,
     sent, psent_x, psent_s, own, part_x, part_s,
     first_m, second_m, chosen_m, weighted_m, hg_buf, act_buf, tg_acc, gate_acc, back_out, back_in,
-    far_term, far_got, slope_pre, act_pre, term, got,
+    far_term, far_got, slope_pre, act_pre, grad_pre, term, got,
     load_sem, pair_send, pair_recv,
     lane_send, lane_recv, ring_send, ring_recv, far_send, far_recv,
 ):
@@ -52,23 +52,6 @@
     up, down = lax.rem(z + 1, n_z), lax.rem(z + n_z - 1, n_z)
     far = lax.rem(z + n_z // 2, n_z)
 
-    barrier = pltpu.get_barrier_semaphore()
-    for other in (far, up, down):
-        pl.semaphore_signal(barrier, inc=1, device_id=(me, other), device_id_type=MESH)
-
-    ahead_x = [lax.rem(cx + k, n_x) * 2 for k in range(n_x)]
-    ahead_y = [lax.rem(cy + k, n_y) * (2 * n_x) for k in range(n_y)]
-    cells = sorted(
-        ((dx, dy_) for dx in range(n_x) for dy_ in range(n_y)),
-        key=lambda cell: -min(cell[0], n_x - cell[0]) - min(cell[1], n_y - cell[1]),
-    )
-    peers = [
-        ahead_y[dy_] + ahead_x[dx] + c
-        for c in (1 - core, core) for dx, dy_ in cells
-    ][:-1]
-    for other in peers:
-        pl.semaphore_signal(barrier, inc=1, device_id=(other, z), device_id_type=MESH)
-
     loads = [
         pltpu.make_async_copy(src, dst, load_sem.at[k])
         for k, (src, dst) in enumerate(
@@ -78,7 +61,28 @@
             )
         )
     ]
-    for k in (4, 5, 6, 0, 1, 2, 3):
+    for k in (4, 5, 6, 0, 1):
+        loads[k].start()
+
+    barrier = pltpu.get_barrier_semaphore()
+    for other in (far, up, down):
+        pl.semaphore_signal(barrier, inc=1, device_id=(me, other), device_id_type=MESH)
+
+    ahead_x = [lax.rem(cx + k, n_x) * 2 for k in range(n_x)]
+    ahead_y = [lax.rem(cy + k, n_y) * (2 * n_x) for k in range(n_y)]
+    cells = (
+        (2, 2), (1, 2), (2, 1), (2, 3), (3, 2), (2, 0), (1, 1), (1, 3),
+        (0, 2), (3, 1), (3, 3), (1, 0), (0, 1), (0, 3), (3, 0), (0, 0),
+    )
+    assert n_x == n_y == 4
+    peers = [
+        ahead_y[dy_] + ahead_x[dx] + c
+        for c in (1 - core, core) for dx, dy_ in cells
+    ][:-1]
+    for other in peers:
+        pl.semaphore_signal(barrier, inc=1, device_id=(other, z), device_id_type=MESH)
+
+    for k in (2, 3):
         loads[k].start()
 
     for k in (4, 5, 6):
@@ -277,9 +281,17 @@
     relay(3)
     gin_ref[...] = dot(hg_buf[above], rows_of(own[:, 0]), 0, 0)
     gout_ref[...] = dot(act_buf[below], rows_of(own[:, 1]), 0, 0)
+    def take(part):
+        whole(3, part).wait_recv()
+        block_s = part_s[:, :, cuts[part]].reshape(rows, width // PARTS)
+        gout_ref[:, cuts[part]] += dot(act_pre[...], block_s, 0, 0)
+        return dot(block_s, wout[units(above), cuts[part]], 1, 1)
+
+    grad_pre[...] = take(0)
+    for part in range(1, PARTS - 1):
+        grad_pre[...] += take(part)
     relay(4)
-    for part in range(PARTS):
-        whole(3, part).wait_recv()
+    active_grad = take(PARTS - 1) + grad_pre[...]
 
     def near(target, store_in, store_out):
         x_p, s_p = rows_of(part_x[...]), rows_of(part_s[...])
@@ -309,12 +321,9 @@
 
         return store
 
-    grad = gout_ref[...] + dot(act_pre[...], rows_of(part_s[...]), 0, 0)
-    to_term(1)(grad[:near_rows])
+    to_term(1)(gout_ref[:near_rows, :])
     ring(1).start()
-    hidden_grad = (
-        dot(rows_of(part_s[...]), wout[units(above), :], 1, 1) * slope_pre[...]
-    ).astype(BF16)
+    hidden_grad = (active_grad * slope_pre[...]).astype(BF16)
     grad = gin_ref[...] + dot(hidden_grad, rows_of(part_x[...]), 0, 0)
     to_term(0)(grad[:near_rows])
     ring(0).start()
@@ -401,7 +410,7 @@
         + [pltpu.VMEM((rows, width), F32), pltpu.VMEM((rows, GATE), F32)]
         + [pltpu.VMEM((n_e, SLOT, width + GATE), BF16)] * 2
         + [pltpu.VMEM((ff // ff_dev, 2, LONG, width), BF16), pltpu.VMEM((2, 7, LONG, width), BF16)]
-        + [pltpu.VMEM((rows, ff_dev), F32), pltpu.VMEM((rows, ff_dev), BF16)]
+        + [pltpu.VMEM((rows, ff_dev), F32), pltpu.VMEM((rows, ff_dev), BF16), pltpu.VMEM((rows, ff_dev), F32)]
         + [pltpu.VMEM((6, ff_dev - LONG, width), BF16)] * 2
         + [pltpu.SemaphoreType.DMA((7,))]
         + [pltpu.SemaphoreType.DMA((1 + 2 * PARTS,))] * 2

time: 94.6 us -> 94.6 us (level)
  no operation moved by 1% of the time
where the time goes in v4:
time: 94.6 us; the launch traced here: 94.5 us
  Pallas kernels  93.7 us (99%)
    pallas_call x1, Pallas kernels, per_device(): pl.pallas_call(functools.partial(kernel, capacity, n_x, n_y), out_shape=(...  92.2 us

profile of v4, /device:TPU:2, one launch (start us, length us, event | category | flops | bytes accessed | tf_op | source)
XLA Modules:
  0.0 94.5 jit_solution(11479808033102636320)
XLA Ops:
  0.6 92.2 %shard_map.102 = (bf16[192,1024]{1,0:T(8,128)(2,1)S(1)}, bf16[2,192]{1,0:T(2,128)(2,1)S(1)}, f32[256,1024]{1,0:T(8,128)S(1)}, f32[256,1024]{1,0:T(8,128)S(1)}) custom-call(bf16[192,1024]{1,0:T(8,128)(2,1)} %tok_hbm.1, bf16[192,1024]{1,0:T(8,128)(2,1)} %dy_hbm.1, s32[2,192]{1,0:T(2,128)} %bitcast.6, s32[1,192]{1,0:T(1,128)} %bitcast.7, ...), custom_call_target="tpu_custom_call" | custom-call | tf_op jit(solution)/shard_map/pallas_call | solution.py:392
  92.8 1.5 %shard_map.103 = (bf16[192,1024]{1,0:T(8,128)(2,1)}, bf16[2,192]{1,0:T(2,128)(2,1)}, f32[256,1024]{1,0:T(8,128)}, f32[256,1024]{1,0:T(8,128)}) custom-call(bf16[192,1024]{1,0:T(8,128)(2,1)S(1)} %get-tuple-element.12.refs_0_, bf16[2,192]{1,0:T(2,128)(2,1)S(1)} %get-tuple-element.13.refs_1_, f32[256,1024]{1,0:T(8,128)S(1)} %get-tuple-element.14.refs_2_, ...), custom_call_target="tpu_custom_call" | custom-call | tf_op jit(solution)/shard_map/pallas_call | solution.py:426
